TPU v7x, 32 devices: a whole 2x2x4 slice. The times are simulated.
32 devices in a mesh: row: 4 (over x, core), col: 4 (over z), layer: 2 (over y).
Axes of the slice: x: 2, y: 2, z: 4, core: 2. Of those that a mesh axis runs over, the one named last changes fastest.
Arguments:
- attn_values: bfloat16 [2048, 8192], P('row', ('layer', 'col')), may hold values from -6 to 6
- out_weight: bfloat16 [8192, 8192], P(('layer', 'row'), 'col'), may hold values from -0.09375 to 0.09375
Outputs:
- projected: bfloat16 [2048, 8192], P('row', ('col', 'layer'))
All inputs are finite; a program needn't handle non-finite values.
Results may differ from a plain program's by a relative error of at most 0.001.
Values may be sent and summed in bfloat16 or wider, within the bound.
A program may use at most 128 MiB of HBM per device.

v0:
```python
import functools

import jax
import jax.numpy as jnp
from jax import lax
from jax.experimental import pallas as pl
from jax.experimental.pallas import tpu as pltpu
from jax.sharding import PartitionSpec as P

TOKEN_CHUNKS = 4
COLUMN_CHUNKS = 8


def last_pieces(depth_w):
    return max(1, min(4, depth_w // 256))


def schedule(token_chunks, column_chunks, col_count):
    events = []
    for t in range(token_chunks):
        for d in range(1, col_count):
            at = (col_count - 1) * t + (1 if d == 1 else d + 1)
            events.append((at, 0, t, d))
    span = (col_count - 1) * token_chunks * 4 / 3
    for j in range(column_chunks - 1):
        events.append((span * (j + 1) / column_chunks, 1, j, 0))
    ordered, clock = [], 0
    for at, kind, first, second in sorted(events, key=lambda e: (e[1], e[2], e[3])):
        if kind == 0:
            clock = max(clock, at)
            at = clock
        ordered.append((at, kind, first, second))
    return sorted(ordered)


def kernel(rows, cols, a_ref, w_ref, o_ref, abuf, wbuf, ysend, yrecv, early, loc_a, loc_w, a_recv, a_right, a_left, w_recv, w_send, p_send, y_recv, y_send):
    r, c, l = lax.axis_index("row"), lax.axis_index("col"), lax.axis_index("layer")
    groups = rows // 2
    core, group = lax.rem(r, 2), r // 2
    partner = 2 * group + 1 - core
    tokens, depth_a = a_ref.shape
    depth_w, width = w_ref.shape
    tt, half = tokens // TOKEN_CHUNKS, width // 2
    nc, jh = width // COLUMN_CHUNKS, COLUMN_CHUNKS // 2
    last, cuts = COLUMN_CHUNKS - 1, last_pieces(depth_w)
    pieces = last + cuts

    def piece(p):
        return (p, 0, depth_w) if p < last else (last, (p - last) * depth_w // cuts, depth_w // cuts)

    def peer(g):
        return 2 * lax.rem(group + g + groups, groups) + core

    def a_at(block, t):
        return abuf.at[block, pl.ds(t * tt, tt), :]

    def w_at(row, p):
        j, start, count = piece(p)
        return wbuf.at[j, pl.ds(pl.multiple_of(row * depth_w + start, count), count), :]

    def own_a(t):
        return pltpu.make_async_copy(a_ref.at[pl.ds(t * tt, tt), :], a_at(c, t), loc_a.at[t])

    def own_w(p):
        j, start, count = piece(p)
        side = 1 - l if j < jh else l
        at = pl.multiple_of(side * half + (j % jh) * nc, nc)
        return pltpu.make_async_copy(w_ref.at[pl.ds(start, count), pl.ds(at, nc)], w_at(r, p), loc_w.at[p])

    def a_copy(block, t, to, sems):
        return pltpu.make_async_remote_copy(a_at(block, t), a_at(block, t), sems.at[t, block], a_recv.at[t, block], device_id={"col": to})

    def w_copy(row, j, to, sem):
        return pltpu.make_async_remote_copy(w_at(row, j), w_at(row, j), sem, w_recv.at[j, row], device_id={"row": to})

    def y_copy(t, j):
        rows_t = pl.ds(t * tt, tt)
        return pltpu.make_async_remote_copy(ysend.at[j, rows_t, :], yrecv.at[j, rows_t, :], y_send.at[t, j], y_recv.at[t, j], device_id={"layer": 1 - l})

    def right(block, t):
        return a_copy(block, t, c + 1, a_right)

    def left(block, t):
        return a_copy(block, t, c - 1, a_left)

    for n in range(max(TOKEN_CHUNKS, pieces)):
        if n < pieces:
            own_w(n).start()
        if n < TOKEN_CHUNKS:
            own_a(n).start()

    has_right, has_left = c < cols - 1, c > 0
    barrier = pltpu.get_barrier_semaphore()

    def greet(device_id):
        pl.semaphore_signal(barrier, inc=1, device_id=device_id)

    greet({"row": partner})
    greet({"layer": 1 - l})
    for g in range(1, groups):
        greet({"row": peer(g)})
    pl.when(has_right)(lambda: greet({"col": c + 1}))
    pl.when(has_left)(lambda: greet({"col": c - 1}))
    pl.semaphore_wait(barrier, 1 + groups + has_right.astype(jnp.int32) + has_left.astype(jnp.int32))

    def send_a(t):
        own_a(t).wait()
        pl.when(has_right)(lambda: right(c, t).start())
        pl.when(has_left)(lambda: left(c, t).start())

    def send_w(j):
        own_w(j).wait()
        for g in range(1, groups):
            w_copy(r, j, peer(g), w_send.at[j, g]).start()
        w_copy(r, j, partner, p_send.at[j, 0]).start()

    send_w(0)
    send_a(0)
    send_a(1)
    for p in range(1, pieces):
        send_w(p)

    def take_a(t, d):
        @pl.when(c >= d)
        def _():
            right(c - d, t).wait_recv()
            pl.when(has_right)(lambda: right(c - d, t).start())

        @pl.when(c + d < cols)
        def _():
            left(c + d, t).wait_recv()
            pl.when(has_left)(lambda: left(c + d, t).start())

        if d == cols - 1 and t + 2 < TOKEN_CHUNKS:
            send_a(t + 2)

    def take_w(j):
        for g in range(1, groups):
            source = peer(-g)
            w_copy(source, j, partner, p_send.at[j, g]).wait_recv()
            w_copy(source, j, partner, p_send.at[j, g]).start()

    def take_partner(j):
        for g in range(groups):
            source = 2 * g + 1 - core
            w_copy(source, j, partner, p_send.at[j, 0]).wait_recv()

    def product(rows_t, j):
        total = jnp.dot(abuf[0, rows_t, :], wbuf[j, pl.ds(0, depth_a), :], preferred_element_type=jnp.float32)
        for block in range(1, cols):
            total += jnp.dot(abuf[block, rows_t, :], wbuf[j, pl.ds(block * depth_a, depth_a), :], preferred_element_type=jnp.float32)
        return total

    def partials(tiles):
        t0, j0 = tiles[0]
        wide = 1 + tiles[-1][1] - j0

        def one(n, carry):
            t, j = t0 + n // wide, j0 + lax.rem(n, wide)
            rows_t = pl.ds(pl.multiple_of(t * tt, tt), tt)
            ysend[j, rows_t, :] = product(rows_t, j)
            return carry

        def send(n, carry):
            y_copy(t0 + n // wide, j0 + lax.rem(n, wide)).start()
            return carry

        lax.fori_loop(0, len(tiles), one, 0)
        lax.fori_loop(0, len(tiles), send, 0)

    def finish(j):
        def one(t, carry):
            rows_t = pl.ds(pl.multiple_of(t * tt * 2, tt * 2), tt * 2)
            y_copy(2 * t, j - jh).wait_recv()
            y_copy(2 * t + 1, j - jh).wait_recv()
            o_ref[rows_t, (j - jh) * nc:(j - jh + 1) * nc] = (product(rows_t, j) + yrecv[j - jh, rows_t, :]).astype(o_ref.dtype)
            return carry

        lax.fori_loop(0, TOKEN_CHUNKS // 2, one, 0)

    def part(j, rows_t, start, count):
        columns = pl.ds(pl.multiple_of(lax.rem(start, depth_a), min(count, depth_a)), count)
        weights = wbuf[j, pl.ds(pl.multiple_of(start, count), count), :]
        return jnp.dot(abuf[start // depth_a, rows_t, columns], weights, preferred_element_type=jnp.float32)

    def each_rows(body):
        def one(t, carry):
            body(pl.ds(pl.multiple_of(t * tt * 2, tt * 2), tt * 2))
            return carry

        lax.fori_loop(0, TOKEN_CHUNKS // 2, one, 0)

    def take_own_rows():
        for h in range(cuts):
            w_copy(partner, last + h, partner, p_send.at[last + h, 0]).wait_recv()
        count = min(depth_w, depth_a)
        for n in range(depth_w // count):
            @each_rows
            def _(rows_t):
                total = part(last, rows_t, r * depth_w + n * count, count) + part(last, rows_t, partner * depth_w + n * count, count)
                early[rows_t, :] = total if n == 0 else early[rows_t, :] + total

    def finish_last():
        count = depth_w // cuts
        for t in range(TOKEN_CHUNKS):
            y_copy(t, jh - 1).wait_recv()
        for h in range(cuts):
            take_w(last + h)
            for g in range(1, groups):
                own, other = peer(-g), peer(-g) + 1 - 2 * core

                @each_rows
                def _(rows_t):
                    early[rows_t, :] += part(last, rows_t, own * depth_w + h * count, count)

                w_copy(other, last + h, partner, p_send.at[last + h, 0]).wait_recv()

                @each_rows
                def _(rows_t):
                    total = early[rows_t, :] + part(last, rows_t, other * depth_w + h * count, count)
                    if h < cuts - 1 or g < groups - 1:
                        early[rows_t, :] = total
                    else:
                        o_ref[rows_t, (jh - 1) * nc:jh * nc] = (total + yrecv[jh - 1, rows_t, :]).astype(o_ref.dtype)

    got_t, got_j, done_own, own_rows = 0, 0, jh, False
    for _, kind, first, second in schedule(TOKEN_CHUNKS, COLUMN_CHUNKS, cols):
        if kind == 0:
            take_a(first, second)
            if second == cols - 1:
                got_t = first + 1
                if got_j:
                    partials([(first, j) for j in range(min(got_j, jh))])
        else:
            if first == last - 1 and got_t == TOKEN_CHUNKS:
                take_own_rows()
                own_rows = True
            take_w(first)
            take_partner(first)
            got_j = first + 1
            if first < jh and got_t:
                partials([(t, first) for t in range(got_t)])
        while got_t == TOKEN_CHUNKS and done_own < got_j:
            finish(done_own)
            done_own += 1
    if not own_rows:
        take_own_rows()
    finish_last()

    for t in range(TOKEN_CHUNKS):
        for block in range(cols):
            @pl.when(has_right & (block <= c))
            def _():
                right(block, t).wait_send()

            @pl.when(has_left & (block >= c))
            def _():
                left(block, t).wait_send()

        for j in range(jh):
            y_copy(t, j).wait_send()
    for p in range(pieces):
        for g in range(groups):
            w_copy(r, p, partner, p_send.at[p, g]).wait_send()
            if g:
                w_copy(r, p, partner, w_send.at[p, g]).wait_send()


def solution(mesh):
    rows, cols = mesh.shape["row"], mesh.shape["col"]

    def shards(attn_values, out_weight):
        tokens, depth_a = attn_values.shape
        depth_w, width = out_weight.shape
        nc, jh = width // COLUMN_CHUNKS, COLUMN_CHUNKS // 2
        pieces = COLUMN_CHUNKS - 1 + last_pieces(depth_w)
        dma = pltpu.SemaphoreType.DMA
        return pl.pallas_call(
            functools.partial(kernel, rows, cols),
            out_shape=jax.ShapeDtypeStruct((tokens, width // 2), jnp.bfloat16),
            in_specs=[pl.BlockSpec(memory_space=pltpu.HBM)] * 2,
            out_specs=pl.BlockSpec(memory_space=pltpu.VMEM),
            scratch_shapes=[
                pltpu.VMEM((cols, tokens, depth_a), jnp.bfloat16),
                pltpu.VMEM((COLUMN_CHUNKS, rows * depth_w, nc), jnp.bfloat16),
                pltpu.VMEM((jh, tokens, nc), jnp.float32),
                pltpu.VMEM((jh, tokens, nc), jnp.float32),
                pltpu.VMEM((tokens, nc), jnp.float32),
                dma((TOKEN_CHUNKS,)),
                dma((pieces,)),
                dma((TOKEN_CHUNKS, cols)),
                dma((TOKEN_CHUNKS, cols)),
                dma((TOKEN_CHUNKS, cols)),
                dma((pieces, rows)),
                dma((pieces, rows // 2)),
                dma((pieces, rows // 2)),
                dma((TOKEN_CHUNKS, jh)),
                dma((TOKEN_CHUNKS, jh)),
            ],
            compiler_params=pltpu.CompilerParams(collective_id=0, has_side_effects=True, vmem_limit_bytes=48 * 2**20),
        )(*(pltpu.with_memory_space_constraint(x, pltpu.HBM) for x in (attn_values, out_weight)))

    in_specs = (P("row", ("layer", "col")), P(("layer", "row"), "col"))
    out_specs = P("row", ("col", "layer"))
    return jax.shard_map(shards, mesh=mesh, in_specs=in_specs, out_specs=out_specs, check_vma=False)
```

profile of v0, /device:TPU:0, one launch (start us, length us, event | category | flops | bytes accessed | tf_op | source)
XLA Modules:
  0.0 99.5 jit_solution(3855061594775070620)
XLA Ops:
  0.0 98.5 %shard_map.28 = bf16[512,1024]{1,0:T(8,128)(2,1)S(1)} custom-call(bf16[512,1024]{1,0:T(8,128)(2,1)} %a_ref.1, bf16[1024,2048]{1,0:T(8,128)(2,1)} %w_ref.1), custom_call_target="tpu_custom_call" | custom-call | tf_op jit(solution)/shard_map/pallas_call | solution.py:278
  98.5 1.0 copy.4
where the time goes:
time: 99.6 us; the launch traced here: 99.5 us
  Pallas kernels  98.5 us (99%)
    pallas_call x1, Pallas kernels, shards(): pl.pallas_call(functools.partial(kernel, rows, cols), out_shape=jax.Shape...  98.5 us

commit v1 on v0

--- a/solution.py
+++ b/solution.py
@@ -266,10 +266,301 @@
                 w_copy(r, p, partner, w_send.at[p, g]).wait_send()
 
 
+PIECES = 16
+SPAN = 250.0
+
+
+def pair_kernel(rows, cols, a_ref, w_ref, o_ref, abuf, wbuf, acc, part, ysend, yrecv, xsend, xrecv, loc_a, loc_w, a_recv, f_send, b_send, c_send, w_send, w_recv, y_send, y_recv, x_send, x_recv):
+    r, c, l = lax.axis_index("row"), lax.axis_index("col"), lax.axis_index("layer")
+    x, core = r // 2, lax.rem(r, 2)
+    partner, peer = 2 * x + 1 - core, 2 * (1 - x) + core
+    step, u, far = 1 - 2 * x, c + x * (cols - 1 - 2 * c), cols - 1
+    own = core + x * (1 - 2 * core)
+    tokens, depth = a_ref.shape
+    half = w_ref.shape[1] // 2
+    tt, nc = tokens // PIECES, wbuf.shape[3]
+    tiles = half // nc
+    lead = min(4, PIECES)
+
+    def rows_at(t, side):
+        return pl.ds(pl.multiple_of((2 * t + side) * tt, tt), tt)
+
+    def rows_of(t):
+        return pl.ds(pl.multiple_of(t * tt, tt), tt)
+
+    def a_at(v, side, t):
+        return abuf.at[v, rows_at(t, side), :]
+
+    def own_a(t):
+        return pltpu.make_async_copy(a_ref.at[rows_of(t), :], a_at(u - u // far, 0, t), loc_a.at[t])
+
+    def own_w(j):
+        side = 1 - l if j < tiles else l
+        at = pl.multiple_of(side * half + (j % tiles) * nc, nc)
+        return pltpu.make_async_copy(w_ref.at[:, pl.ds(at, nc)], wbuf.at[own, j], loc_w.at[j])
+
+    def w_copy(slot, j):
+        return pltpu.make_async_remote_copy(wbuf.at[slot, j], wbuf.at[slot, j], w_send.at[j], w_recv.at[j], device_id={"row": partner})
+
+    def ahead(v, side, t):
+        return pltpu.make_async_remote_copy(a_at(v, side, t), a_at(v, side, t), f_send.at[v + 2 * side, t], a_recv.at[v, side, t], device_id={"col": c + step})
+
+    def back(v, side, t):
+        return pltpu.make_async_remote_copy(a_at(v, side, t), a_at(v, side, t), b_send.at[v - 1 + 2 * side, t], a_recv.at[v, side, t], device_id={"col": c - step})
+
+    def across(t):
+        to = 1 - u // far
+        return pltpu.make_async_remote_copy(a_at(2, 0, t), a_at(to, 1, t), c_send.at[t], a_recv.at[to, 1, t], device_id={"row": peer})
+
+    def y_copy(t, side):
+        at = rows_at(t, side)
+        return pltpu.make_async_remote_copy(ysend.at[at, :], yrecv.at[at, :], y_send.at[t, side], y_recv.at[t, side], device_id={"layer": 1 - l})
+
+    def x_copy(t):
+        at = rows_of(t)
+        return pltpu.make_async_remote_copy(xsend.at[at, :], xrecv.at[at, :], x_send.at[t], x_recv.at[t], device_id={"row": peer})
+
+    def take(v, side, t):
+        ahead(v, side, t).wait_recv()
+
+    def within(t, body):
+        pl.when(t < PIECES)(lambda: body(t))
+
+    for t in range(PIECES):
+        own_a(t).start()
+    for j in range(2 * tiles):
+        own_w(j).start()
+
+    has_next, has_last = u < far, u > 0
+    barrier = pltpu.get_barrier_semaphore()
+
+    def greet(device_id):
+        pl.semaphore_signal(barrier, inc=1, device_id=device_id)
+
+    greet({"row": partner})
+    greet({"row": peer})
+    greet({"layer": 1 - l})
+    pl.when(has_next)(lambda: greet({"col": c + step}))
+    pl.when(has_last)(lambda: greet({"col": c - step}))
+    pl.semaphore_wait(barrier, 3 + has_next.astype(jnp.int32) + has_last.astype(jnp.int32))
+
+    def send_first(t):
+        own_a(t).wait()
+        ahead(0, 0, t).start()
+
+    def send_second(t):
+        own_a(t).wait()
+        ahead(1, 0, t).start()
+        back(1, 0, t).start()
+
+    @pl.when(u == 0)
+    def _():
+        for t in range(lead):
+            send_first(t)
+
+    @pl.when(u == 1)
+    def _():
+        for t in range(lead):
+            send_second(t)
+
+    @pl.when(u == 2)
+    def _():
+        for t in range(PIECES):
+            own_a(t).wait()
+            across(t).start()
+            back(2, 0, t).start()
+
+    @pl.when(u == far)
+    def _():
+        for t in range(PIECES):
+            own_a(t).wait()
+            across(t).start()
+
+    for j in range(2 * tiles):
+        own_w(j).wait()
+        w_copy(own, j).start()
+
+    def pass_first(t):
+        take(0, 1, t)
+        ahead(0, 1, t).start()
+
+    def pass_back(t):
+        take(2, 0, t)
+        back(2, 0, t).start()
+        across(t).start()
+        take(1, 1, t)
+        back(1, 1, t).start()
+
+    def pass_on(t):
+        take(0, 0, t)
+        ahead(0, 0, t).start()
+        take(0, 1, t)
+        ahead(0, 1, t).start()
+
+    @pl.when(u == 0)
+    def _():
+        for t in range(3):
+            pass_first(t)
+
+    @pl.when(u == 1)
+    def _():
+        for t in range(3):
+            pass_back(t)
+        for t in range(2):
+            pass_on(t)
+
+    def gather(t):
+        @pl.when(u == 0)
+        def _():
+            within(t + 3, pass_first)
+            within(t + lead, send_first)
+            take(1, 0, t)
+            take(2, 0, t)
+            across(t).start()
+            take(1, 1, t)
+
+        @pl.when(u == 1)
+        def _():
+            within(t + 3, pass_back)
+            within(t + lead, send_second)
+            within(t + 2, pass_on)
+
+        @pl.when(u == 2)
+        def _():
+            for v, side in ((1, 0), (0, 0), (0, 1)):
+                take(v, side, t)
+                ahead(v, side, t).start()
+            take(1, 1, t)
+
+        @pl.when(u == far)
+        def _():
+            for v, side in ((1, 0), (0, 0), (0, 1), (1, 1)):
+                take(v, side, t)
+
+    def encode(ref, at, value):
+        scale = jnp.maximum(1.01 * jnp.max(jnp.abs(value), axis=1, keepdims=True), 1e-30).astype(jnp.bfloat16)
+        level = jnp.exp2(jnp.abs(value) * (SPAN / scale.astype(jnp.float32)) - SPAN / 2)
+        ref[at, :half] = jnp.where(value < 0, -level, level).astype(jnp.bfloat16)
+        ref[at, half:] = jnp.broadcast_to(scale, (value.shape[0], ref.shape[1] - half))
+
+    def decode(ref, at):
+        level = ref[at, :half].astype(jnp.float32)
+        scale = ref[at, half:half + 1].astype(jnp.float32)
+        share = jnp.log2(jnp.abs(level)) * (1 / SPAN) + 0.5
+        return jnp.where(level < 0, -share, share) * scale
+
+    def multiply(t):
+        at = pl.ds(pl.multiple_of(2 * t * tt, 2 * tt), 2 * tt)
+        first, second = abuf[0, at, :], abuf[1, at, :]
+        for j in range(2 * tiles):
+            @pl.when(t == 0)
+            def _():
+                w_copy(1 - own, j).wait_recv()
+
+            total = jnp.dot(first, wbuf[0, j], preferred_element_type=jnp.float32) + jnp.dot(second, wbuf[1, j], preferred_element_type=jnp.float32)
+            columns = pl.ds((j % tiles) * nc, nc)
+            if j < tiles:
+                part[:, columns] = total
+            else:
+                acc[at, columns] = total
+        for side in (1, 0):
+            encode(ysend, rows_at(t, side), part[side * tt:(side + 1) * tt, :])
+        for side in (1, 0):
+            y_copy(t, side).start()
+
+    def reduce_y(t):
+        y_copy(t, 1).wait_recv()
+        at = rows_at(t, 1)
+        encode(xsend, rows_of(t), acc[at, :] + decode(yrecv, at))
+        x_copy(t).start()
+        y_copy(t, 0).wait_recv()
+        at = rows_at(t, 0)
+        acc[at, :] += decode(yrecv, at)
+
+    def reduce_x(t):
+        x_copy(t).wait_recv()
+        o_ref[rows_of(t), :] = (acc[rows_at(t, 0), :] + decode(xrecv, rows_of(t))).astype(o_ref.dtype)
+
+    def one(t, carry):
+        gather(t)
+        multiply(t)
+        pl.when(t >= 2)(lambda: reduce_y(t - 2))
+        pl.when(t >= 3)(lambda: reduce_x(t - 3))
+        return carry
+
+    lax.fori_loop(0, PIECES, one, 0)
+    reduce_y(PIECES - 2)
+    reduce_y(PIECES - 1)
+    for t in range(PIECES - 3, PIECES):
+        reduce_x(t)
+
+    def settle(t, carry):
+        @pl.when(has_next)
+        def _():
+            ahead(0, 0, t).wait_send()
+            ahead(0, 1, t).wait_send()
+            pl.when(has_last)(lambda: ahead(1, 0, t).wait_send())
+
+        @pl.when(u == 1)
+        def _():
+            back(1, 0, t).wait_send()
+            back(1, 1, t).wait_send()
+
+        pl.when(has_last & has_next)(lambda: back(2, 0, t).wait_send())
+        across(t).wait_send()
+        y_copy(t, 0).wait_send()
+        y_copy(t, 1).wait_send()
+        x_copy(t).wait_send()
+        return carry
+
+    lax.fori_loop(0, PIECES, settle, 0)
+    for j in range(2 * tiles):
+        w_copy(own, j).wait_send()
+
+
+def pair_call(rows, cols, attn_values, out_weight):
+    tokens, depth = attn_values.shape
+    width = out_weight.shape[1]
+    half = width // 2
+    nc = half // 4
+    dma = pltpu.SemaphoreType.DMA
+    return pl.pallas_call(
+        functools.partial(pair_kernel, rows, cols),
+        out_shape=jax.ShapeDtypeStruct((tokens, half), jnp.bfloat16),
+        in_specs=[pl.BlockSpec(memory_space=pltpu.HBM)] * 2,
+        out_specs=pl.BlockSpec(memory_space=pltpu.VMEM),
+        scratch_shapes=[
+            pltpu.VMEM((3, 2 * tokens, depth), jnp.bfloat16),
+            pltpu.VMEM((2, width // nc, depth, nc), jnp.bfloat16),
+            pltpu.VMEM((2 * tokens, half), jnp.float32),
+            pltpu.VMEM((2 * tokens // PIECES, half), jnp.float32),
+            pltpu.VMEM((2 * tokens, half + 128), jnp.bfloat16),
+            pltpu.VMEM((2 * tokens, half + 128), jnp.bfloat16),
+            pltpu.VMEM((tokens, half + 128), jnp.bfloat16),
+            pltpu.VMEM((tokens, half + 128), jnp.bfloat16),
+            dma((PIECES,)),
+            dma((width // nc,)),
+            dma((3, 2, PIECES)),
+            dma((3, PIECES)),
+            dma((3, PIECES)),
+            dma((PIECES,)),
+            dma((width // nc,)),
+            dma((width // nc,)),
+            dma((PIECES, 2)),
+            dma((PIECES, 2)),
+            dma((PIECES,)),
+            dma((PIECES,)),
+        ],
+        compiler_params=pltpu.CompilerParams(collective_id=1, has_side_effects=True, vmem_limit_bytes=48 * 2**20),
+    )(*(pltpu.with_memory_space_constraint(v, pltpu.HBM) for v in (attn_values, out_weight)))
+
+
 def solution(mesh):
     rows, cols = mesh.shape["row"], mesh.shape["col"]
 
     def shards(attn_values, out_weight):
+        if rows == cols == 4:
+            return pair_call(rows, cols, attn_values, out_weight)
         tokens, depth_a = attn_values.shape
         depth_w, width = out_weight.shape
         nc, jh = width // COLUMN_CHUNKS, COLUMN_CHUNKS // 2

time: 99.6 us -> 117 us (1.17)
  Pallas kernels: 98.5 us -> 116 us
    pallas_call x1, Pallas kernels: 98.5 us -> 116 us  [pair_call(): pl.pallas_call(functools.partial(pair_kernel, rows, cols), out_shape=jax....]
where the time goes in v1:
time: 117 us
  Pallas kernels  116 us (99%)
    pallas_call x1, Pallas kernels, pair_call(): pl.pallas_call(functools.partial(pair_kernel, rows, cols), out_shape=jax....  116 us

profile of v1, /device:TPU:0, one launch (start us, length us, event | category | flops | bytes accessed | tf_op | source)
XLA Modules:
  0.0 116.9 jit_solution(5650862939168593295)
XLA Ops:
  0.0 115.9 %shard_map.28 = bf16[512,1024]{1,0:T(8,128)(2,1)S(1)} custom-call(bf16[512,1024]{1,0:T(8,128)(2,1)} %a_ref.1, bf16[1024,2048]{1,0:T(8,128)(2,1)} %w_ref.1), custom_call_target="tpu_custom_call" | custom-call | tf_op jit(solution)/shard_map/pallas_call | solution.py:527
  116.0 1.0 copy.4

commit v2 on v1

--- a/solution.py
+++ b/solution.py
@@ -267,6 +267,12 @@
 
 
 PIECES = 16
+FILL = 6
+FILL_BACK = 3
+LEAD = 2
+LAG_O = 1
+LAG_Y = 2
+LAG_X = 5
 SPAN = 250.0
 
 
@@ -280,10 +286,10 @@
     half = w_ref.shape[1] // 2
     tt, nc = tokens // PIECES, wbuf.shape[3]
     tiles = half // nc
-    lead = min(4, PIECES)
 
     def rows_at(t, side):
-        return pl.ds(pl.multiple_of((2 * t + side) * tt, tt), tt)
+        at = 2 * t if side == 0 else 2 * lax.rem(t + PIECES - LEAD, PIECES) + 1
+        return pl.ds(pl.multiple_of(at * tt, tt), tt)
 
     def rows_of(t):
         return pl.ds(pl.multiple_of(t * tt, tt), tt)
@@ -291,40 +297,53 @@
     def a_at(v, side, t):
         return abuf.at[v, rows_at(t, side), :]
 
+    def a_all(v):
+        return abuf.at[v, pl.ds(0, tokens), :]
+
     def own_a(t):
-        return pltpu.make_async_copy(a_ref.at[rows_of(t), :], a_at(u - u // far, 0, t), loc_a.at[t])
+        return pltpu.make_async_copy(a_ref.at[rows_of(t), :], a_at(u - u // far, 0, t), loc_a)
 
     def own_w(j):
         side = 1 - l if j < tiles else l
         at = pl.multiple_of(side * half + (j % tiles) * nc, nc)
         return pltpu.make_async_copy(w_ref.at[:, pl.ds(at, nc)], wbuf.at[own, j], loc_w.at[j])
 
+    def remote(source, target, sent, got, **device):
+        return pltpu.make_async_remote_copy(source, target, sent, got, device_id=device)
+
     def w_copy(slot, j):
-        return pltpu.make_async_remote_copy(wbuf.at[slot, j], wbuf.at[slot, j], w_send.at[j], w_recv.at[j], device_id={"row": partner})
+        return remote(wbuf.at[slot, j], wbuf.at[slot, j], w_send, w_recv, row=partner)
+
+    def w_all(slot):
+        return remote(wbuf.at[slot], wbuf.at[slot], w_send, w_recv, row=partner)
 
     def ahead(v, side, t):
-        return pltpu.make_async_remote_copy(a_at(v, side, t), a_at(v, side, t), f_send.at[v + 2 * side, t], a_recv.at[v, side, t], device_id={"col": c + step})
+        return remote(a_at(v, side, t), a_at(v, side, t), f_send.at[v + 2 * side], a_recv.at[v + 3 * side, t], col=c + step)
 
     def back(v, side, t):
-        return pltpu.make_async_remote_copy(a_at(v, side, t), a_at(v, side, t), b_send.at[v - 1 + 2 * side, t], a_recv.at[v, side, t], device_id={"col": c - step})
+        return remote(a_at(v, side, t), a_at(v, side, t), b_send.at[v - 1 + 2 * side], a_recv.at[v + 3 * side, t], col=c - step)
 
     def across(t):
         to = 1 - u // far
-        return pltpu.make_async_remote_copy(a_at(2, 0, t), a_at(to, 1, t), c_send.at[t], a_recv.at[to, 1, t], device_id={"row": peer})
+        return remote(a_at(2, 0, t), a_at(to, 1, t), c_send, a_recv.at[to + 3, t], row=peer)
 
     def y_copy(t, side):
         at = rows_at(t, side)
-        return pltpu.make_async_remote_copy(ysend.at[at, :], yrecv.at[at, :], y_send.at[t, side], y_recv.at[t, side], device_id={"layer": 1 - l})
+        return remote(ysend.at[at, :], yrecv.at[at, :], y_send, y_recv.at[t, side], layer=1 - l)
 
     def x_copy(t):
         at = rows_of(t)
-        return pltpu.make_async_remote_copy(xsend.at[at, :], xrecv.at[at, :], x_send.at[t], x_recv.at[t], device_id={"row": peer})
+        return remote(xsend.at[at, :], xrecv.at[at, :], x_send, x_recv.at[t], row=peer)
 
     def take(v, side, t):
         ahead(v, side, t).wait_recv()
 
-    def within(t, body):
-        pl.when(t < PIECES)(lambda: body(t))
+    def within(first, t, body):
+        if isinstance(t, int):
+            if first <= t < PIECES:
+                body(t)
+        else:
+            pl.when((t >= first) & (t < PIECES))(lambda: body(t))
 
     for t in range(PIECES):
         own_a(t).start()
@@ -344,45 +363,61 @@
     pl.when(has_last)(lambda: greet({"col": c - step}))
     pl.semaphore_wait(barrier, 3 + has_next.astype(jnp.int32) + has_last.astype(jnp.int32))
 
+    pltpu.make_async_copy(a_ref, a_all(u - u // far), loc_a).wait()
+
     def send_first(t):
-        own_a(t).wait()
         ahead(0, 0, t).start()
 
-    def send_second(t):
-        own_a(t).wait()
+    def send_ahead(t):
         ahead(1, 0, t).start()
+
+    def send_back(t):
         back(1, 0, t).start()
 
+    def each(start, stop, body):
+        def one(t, carry):
+            body(t)
+            return carry
+
+        lax.fori_loop(start, stop, one, 0)
+
     @pl.when(u == 0)
     def _():
-        for t in range(lead):
-            send_first(t)
+        each(0, 2, send_first)
 
     @pl.when(u == 1)
     def _():
-        for t in range(lead):
-            send_second(t)
+        for t in range(FILL):
+            send_ahead(t)
+            if t < FILL_BACK:
+                send_back(t)
 
     @pl.when(u == 2)
     def _():
-        for t in range(PIECES):
-            own_a(t).wait()
+        def both(t):
             across(t).start()
             back(2, 0, t).start()
 
+        each(0, PIECES, both)
+
     @pl.when(u == far)
     def _():
-        for t in range(PIECES):
-            own_a(t).wait()
-            across(t).start()
+        each(0, PIECES, lambda t: across(t).start())
 
     for j in range(2 * tiles):
         own_w(j).wait()
         w_copy(own, j).start()
 
-    def pass_first(t):
-        take(0, 1, t)
-        ahead(0, 1, t).start()
+    def on(v, side):
+        def body(t):
+            take(v, side, t)
+            ahead(v, side, t).start()
+
+        return body
+
+    def cross(t):
+        take(2, 0, t)
+        across(t).start()
 
     def pass_back(t):
         take(2, 0, t)
@@ -391,51 +426,55 @@
         take(1, 1, t)
         back(1, 1, t).start()
 
-    def pass_on(t):
-        take(0, 0, t)
-        ahead(0, 0, t).start()
-        take(0, 1, t)
-        ahead(0, 1, t).start()
-
     @pl.when(u == 0)
     def _():
-        for t in range(3):
-            pass_first(t)
+        for t in range(4):
+            on(0, 1)(t)
+            if t >= 2:
+                send_first(t)
 
     @pl.when(u == 1)
     def _():
         for t in range(3):
             pass_back(t)
         for t in range(2):
-            pass_on(t)
+            on(0, 1)(t)
+
+    @pl.when(u == 2)
+    def _():
+        for t in range(FILL):
+            on(1, 0)(t)
 
     def gather(t):
         @pl.when(u == 0)
         def _():
-            within(t + 3, pass_first)
-            within(t + lead, send_first)
-            take(1, 0, t)
-            take(2, 0, t)
-            across(t).start()
-            take(1, 1, t)
+            within(0, t + LEAD, cross)
+            within(4, t + LEAD + 4, on(0, 1))
+            within(4, t + 4, send_first)
+            within(0, t + LEAD, lambda t: take(1, 1, t))
+            within(0, t, lambda t: take(1, 0, t))
 
         @pl.when(u == 1)
         def _():
-            within(t + 3, pass_back)
-            within(t + lead, send_second)
-            within(t + 2, pass_on)
+            within(3, t + LEAD + 3, pass_back)
+            within(FILL_BACK, t + 3, send_back)
+            within(2, t + LEAD + 2, on(0, 1))
+            within(0, t + 2, on(0, 0))
+            within(FILL, t + 2, send_ahead)
 
         @pl.when(u == 2)
         def _():
-            for v, side in ((1, 0), (0, 0), (0, 1)):
-                take(v, side, t)
-                ahead(v, side, t).start()
-            take(1, 1, t)
+            within(0, t + LEAD, on(0, 1))
+            within(0, t, on(0, 0))
+            within(FILL, t, on(1, 0))
+            within(0, t + LEAD, lambda t: take(1, 1, t))
 
         @pl.when(u == far)
         def _():
-            for v, side in ((1, 0), (0, 0), (0, 1), (1, 1)):
-                take(v, side, t)
+            within(0, t + LEAD, lambda t: take(0, 1, t))
+            within(0, t + LEAD, lambda t: take(1, 1, t))
+            within(0, t, lambda t: take(0, 0, t))
+            within(0, t, lambda t: take(1, 0, t))
 
     def encode(ref, at, value):
         scale = jnp.maximum(1.01 * jnp.max(jnp.abs(value), axis=1, keepdims=True), 1e-30).astype(jnp.bfloat16)
@@ -449,73 +488,81 @@
         share = jnp.log2(jnp.abs(level)) * (1 / SPAN) + 0.5
         return jnp.where(level < 0, -share, share) * scale
 
-    def multiply(t):
-        at = pl.ds(pl.multiple_of(2 * t * tt, 2 * tt), 2 * tt)
+    def multiply(at, sends):
         first, second = abuf[0, at, :], abuf[1, at, :]
-        for j in range(2 * tiles):
-            @pl.when(t == 0)
-            def _():
-                w_copy(1 - own, j).wait_recv()
-
-            total = jnp.dot(first, wbuf[0, j], preferred_element_type=jnp.float32) + jnp.dot(second, wbuf[1, j], preferred_element_type=jnp.float32)
-            columns = pl.ds((j % tiles) * nc, nc)
-            if j < tiles:
-                part[:, columns] = total
-            else:
-                acc[at, columns] = total
-        for side in (1, 0):
-            encode(ysend, rows_at(t, side), part[side * tt:(side + 1) * tt, :])
-        for side in (1, 0):
+
+        def product(j):
+            return jnp.dot(first, wbuf[0, j], preferred_element_type=jnp.float32) + jnp.dot(second, wbuf[1, j], preferred_element_type=jnp.float32)
+
+        for j in range(tiles):
+            part[:at.size, j * nc:(j + 1) * nc] = product(j)
+        for t, side, start in sends:
+            encode(ysend, rows_at(t, side), part[start:start + tt, :])
+        for t, side, start in sends:
             y_copy(t, side).start()
-
-    def reduce_y(t):
+        for j in range(tiles):
+            acc[at, j * nc:(j + 1) * nc] = product(tiles + j)
+
+    def reduce_other(t):
         y_copy(t, 1).wait_recv()
         at = rows_at(t, 1)
         encode(xsend, rows_of(t), acc[at, :] + decode(yrecv, at))
         x_copy(t).start()
+
+    def reduce_own(t):
         y_copy(t, 0).wait_recv()
         at = rows_at(t, 0)
         acc[at, :] += decode(yrecv, at)
 
-    def reduce_x(t):
+    def finish(t):
         x_copy(t).wait_recv()
         o_ref[rows_of(t), :] = (acc[rows_at(t, 0), :] + decode(xrecv, rows_of(t))).astype(o_ref.dtype)
 
-    def one(t, carry):
+    def reduce(t):
+        within(0, t + LEAD - 1 - LAG_O, reduce_other)
+        within(0, t - LAG_Y, reduce_own)
+        within(0, t - LAG_X, finish)
+
+    def early(t):
         gather(t)
-        multiply(t)
-        pl.when(t >= 2)(lambda: reduce_y(t - 2))
-        pl.when(t >= 3)(lambda: reduce_x(t - 3))
-        return carry
-
-    lax.fori_loop(0, PIECES, one, 0)
-    reduce_y(PIECES - 2)
-    reduce_y(PIECES - 1)
-    for t in range(PIECES - 3, PIECES):
-        reduce_x(t)
-
-    def settle(t, carry):
-        @pl.when(has_next)
-        def _():
-            ahead(0, 0, t).wait_send()
-            ahead(0, 1, t).wait_send()
-            pl.when(has_last)(lambda: ahead(1, 0, t).wait_send())
-
-        @pl.when(u == 1)
-        def _():
-            back(1, 0, t).wait_send()
-            back(1, 1, t).wait_send()
-
-        pl.when(has_last & has_next)(lambda: back(2, 0, t).wait_send())
-        across(t).wait_send()
-        y_copy(t, 0).wait_send()
-        y_copy(t, 1).wait_send()
-        x_copy(t).wait_send()
-        return carry
-
-    lax.fori_loop(0, PIECES, settle, 0)
-    for j in range(2 * tiles):
-        w_copy(own, j).wait_send()
+        multiply(rows_at(t + LEAD, 1), [(t + LEAD, 1, 0)])
+        reduce(t)
+
+    def steady(t):
+        gather(t)
+        multiply(pl.ds(pl.multiple_of(2 * t * tt, 2 * tt), 2 * tt), [(t + LEAD, 1, tt), (t, 0, 0)])
+        reduce(t)
+
+    def late(t):
+        gather(t)
+        multiply(rows_at(t, 0), [(t, 0, 0)])
+        reduce(t)
+
+    w_all(1 - own).wait_recv()
+    each(-LEAD, 0, early)
+    each(0, PIECES - LEAD, steady)
+    each(PIECES - LEAD, PIECES, late)
+    each(PIECES, PIECES + LAG_X, reduce)
+
+    def sent(sem):
+        remote(a_all(0), a_all(0), sem, a_recv.at[0, 0], row=peer).wait_send()
+
+    @pl.when(has_next)
+    def _():
+        sent(f_send.at[0])
+        sent(f_send.at[2])
+        pl.when(has_last)(lambda: sent(f_send.at[1]))
+
+    @pl.when(u == 1)
+    def _():
+        sent(b_send.at[0])
+        sent(b_send.at[2])
+
+    pl.when(has_last & has_next)(lambda: sent(b_send.at[1]))
+    sent(c_send)
+    remote(ysend, yrecv, y_send, y_recv.at[0, 0], layer=1 - l).wait_send()
+    remote(xsend, xrecv, x_send, x_recv.at[0], row=peer).wait_send()
+    w_all(own).wait_send()
 
 
 def pair_call(rows, cols, attn_values, out_weight):
@@ -538,17 +585,17 @@
             pltpu.VMEM((2 * tokens, half + 128), jnp.bfloat16),
             pltpu.VMEM((tokens, half + 128), jnp.bfloat16),
             pltpu.VMEM((tokens, half + 128), jnp.bfloat16),
-            dma((PIECES,)),
+            dma,
             dma((width // nc,)),
-            dma((3, 2, PIECES)),
-            dma((3, PIECES)),
-            dma((3, PIECES)),
-            dma((PIECES,)),
-            dma((width // nc,)),
-            dma((width // nc,)),
+            dma((5, PIECES)),
+            dma((3,)),
+            dma((3,)),
+            dma,
+            dma,
+            dma,
+            dma,
             dma((PIECES, 2)),
-            dma((PIECES, 2)),
-            dma((PIECES,)),
+            dma,
             dma((PIECES,)),
         ],
         compiler_params=pltpu.CompilerParams(collective_id=1, has_side_effects=True, vmem_limit_bytes=48 * 2**20),

time: 117 us -> 87 us (0.74)
  Pallas kernels: 116 us -> 85.9 us
    pallas_call x1, Pallas kernels: 116 us -> 85.9 us  [pair_call(): pl.pallas_call(functools.partial(pair_kernel, rows, cols), out_shape=jax....]
where the time goes in v2:
time: 87 us; the launch traced here: 86.9 us
  Pallas kernels  85.9 us (99%)
  local copies, waits for them, and re-layouts  0.97 us (1%)
    pallas_call x1, Pallas kernels, pair_call(): pl.pallas_call(functools.partial(pair_kernel, rows, cols), out_shape=jax....  85.9 us

profile of v2, /device:TPU:0, one launch (start us, length us, event | category | flops | bytes accessed | tf_op | source)
XLA Modules:
  0.0 86.9 jit_solution(972077191683278744)
XLA Ops:
  0.0 85.9 %shard_map.28 = bf16[512,1024]{1,0:T(8,128)(2,1)S(1)} custom-call(bf16[512,1024]{1,0:T(8,128)(2,1)} %a_ref.1, bf16[1024,2048]{1,0:T(8,128)(2,1)} %w_ref.1), custom_call_target="tpu_custom_call" | custom-call | tf_op jit(solution)/shard_map/pallas_call | solution.py:574
  85.9 1.0 %copy.4 = bf16[512,1024]{1,0:T(8,128)(2,1)} copy(bf16[512,1024]{1,0:T(8,128)(2,1)S(1)} %shard_map.28) | data formatting | bytes 2097152

commit v3 on v2

--- a/solution.py
+++ b/solution.py
@@ -269,7 +269,7 @@
 PIECES = 16
 FILL = 6
 FILL_BACK = 3
-LEAD = 2
+LEAD = 3
 LAG_O = 1
 LAG_Y = 2
 LAG_X = 5
@@ -306,13 +306,10 @@
     def own_w(j):
         side = 1 - l if j < tiles else l
         at = pl.multiple_of(side * half + (j % tiles) * nc, nc)
-        return pltpu.make_async_copy(w_ref.at[:, pl.ds(at, nc)], wbuf.at[own, j], loc_w.at[j])
+        return pltpu.make_async_copy(w_ref.at[:, pl.ds(at, nc)], wbuf.at[own, j], loc_w)
 
     def remote(source, target, sent, got, **device):
         return pltpu.make_async_remote_copy(source, target, sent, got, device_id=device)
-
-    def w_copy(slot, j):
-        return remote(wbuf.at[slot, j], wbuf.at[slot, j], w_send, w_recv, row=partner)
 
     def w_all(slot):
         return remote(wbuf.at[slot], wbuf.at[slot], w_send, w_recv, row=partner)
@@ -347,8 +344,6 @@
 
     for t in range(PIECES):
         own_a(t).start()
-    for j in range(2 * tiles):
-        own_w(j).start()
 
     has_next, has_last = u < far, u > 0
     barrier = pltpu.get_barrier_semaphore()
@@ -405,8 +400,9 @@
         each(0, PIECES, lambda t: across(t).start())
 
     for j in range(2 * tiles):
-        own_w(j).wait()
-        w_copy(own, j).start()
+        own_w(j).start()
+    pltpu.make_async_copy(wbuf.at[1 - own], wbuf.at[own], loc_w).wait()
+    w_all(own).start()
 
     def on(v, side):
         def body(t):
@@ -488,7 +484,7 @@
         share = jnp.log2(jnp.abs(level)) * (1 / SPAN) + 0.5
         return jnp.where(level < 0, -share, share) * scale
 
-    def multiply(at, sends):
+    def multiply(at, sends, between=None):
         first, second = abuf[0, at, :], abuf[1, at, :]
 
         def product(j):
@@ -500,6 +496,8 @@
             encode(ysend, rows_at(t, side), part[start:start + tt, :])
         for t, side, start in sends:
             y_copy(t, side).start()
+        if between:
+            between()
         for j in range(tiles):
             acc[at, j * nc:(j + 1) * nc] = product(tiles + j)
 
@@ -518,10 +516,13 @@
         x_copy(t).wait_recv()
         o_ref[rows_of(t), :] = (acc[rows_at(t, 0), :] + decode(xrecv, rows_of(t))).astype(o_ref.dtype)
 
+    def finish_own(t):
+        within(0, t - LAG_Y, reduce_own)
+        within(0, t - LAG_X, finish)
+
     def reduce(t):
         within(0, t + LEAD - 1 - LAG_O, reduce_other)
-        within(0, t - LAG_Y, reduce_own)
-        within(0, t - LAG_X, finish)
+        finish_own(t)
 
     def early(t):
         gather(t)
@@ -535,14 +536,14 @@
 
     def late(t):
         gather(t)
-        multiply(rows_at(t, 0), [(t, 0, 0)])
-        reduce(t)
+        multiply(rows_at(t, 0), [(t, 0, 0)], lambda: within(0, t + LEAD - 1 - LAG_O, reduce_other))
+        finish_own(t)
 
     w_all(1 - own).wait_recv()
     each(-LEAD, 0, early)
     each(0, PIECES - LEAD, steady)
     each(PIECES - LEAD, PIECES, late)
-    each(PIECES, PIECES + LAG_X, reduce)
+    each(PIECES, PIECES + LAG_X, finish_own)
 
     def sent(sem):
         remote(a_all(0), a_all(0), sem, a_recv.at[0, 0], row=peer).wait_send()
@@ -586,7 +587,7 @@
             pltpu.VMEM((tokens, half + 128), jnp.bfloat16),
             pltpu.VMEM((tokens, half + 128), jnp.bfloat16),
             dma,
-            dma((width // nc,)),
+            dma,
             dma((5, PIECES)),
             dma((3,)),
             dma((3,)),

time: 87 us -> 84.7 us (0.974)
  Pallas kernels: 85.9 us -> 83 us
    pallas_call x1, Pallas kernels: 85.9 us -> 83 us  [pair_call(): pl.pallas_call(functools.partial(pair_kernel, rows, cols), out_shape=jax....]
where the time goes in v3:
time: 84.7 us; the launch traced here: 84 us
  Pallas kernels  83 us (98%)
  local copies, waits for them, and re-layouts  0.97 us (1%)
    pallas_call x1, Pallas kernels, pair_call(): pl.pallas_call(functools.partial(pair_kernel, rows, cols), out_shape=jax....  83 us

profile of v3, /device:TPU:0, one launch (start us, length us, event | category | flops | bytes accessed | tf_op | source)
XLA Modules:
  0.0 84.0 jit_solution(12063899737339677145)
XLA Ops:
  0.0 83.0 %shard_map.28 = bf16[512,1024]{1,0:T(8,128)(2,1)S(1)} custom-call(bf16[512,1024]{1,0:T(8,128)(2,1)} %a_ref.1, bf16[1024,2048]{1,0:T(8,128)(2,1)} %w_ref.1), custom_call_target="tpu_custom_call" | custom-call | tf_op jit(solution)/shard_map/pallas_call | solution.py:575
  83.0 1.0 %copy.4 = bf16[512,1024]{1,0:T(8,128)(2,1)} copy(bf16[512,1024]{1,0:T(8,128)(2,1)S(1)} %shard_map.28) | data formatting | bytes 2097152

commit v4 on v3

--- a/solution.py
+++ b/solution.py
@@ -267,6 +267,8 @@
 
 
 PIECES = 16
+DETOURS = ((12, 2, 5), (14, 4, 7))
+SHORT = 2
 FILL = 6
 FILL_BACK = 3
 LEAD = 3
@@ -315,14 +317,30 @@
         return remote(wbuf.at[slot], wbuf.at[slot], w_send, w_recv, row=partner)
 
     def ahead(v, side, t):
-        return remote(a_at(v, side, t), a_at(v, side, t), f_send.at[v + 2 * side], a_recv.at[v + 3 * side, t], col=c + step)
+        return remote(a_at(v, side, t), a_at(v, side, t), f_send.at[v + 2 * side], a_recv.at[v + 2 * side, t], col=c + step)
 
     def back(v, side, t):
-        return remote(a_at(v, side, t), a_at(v, side, t), b_send.at[v - 1 + 2 * side], a_recv.at[v + 3 * side, t], col=c - step)
+        return remote(a_at(v, side, t), a_at(v, side, t), b_send.at[v - 1 + 2 * side], a_recv.at[u - 1 if v == 2 else v + 2 * side, t], col=c - step)
 
     def across(t):
         to = 1 - u // far
-        return remote(a_at(2, 0, t), a_at(to, 1, t), c_send, a_recv.at[to + 3, t], row=peer)
+        return remote(a_at(2, 0, t), a_at(to, 1, t), c_send, a_recv.at[to + 2, t], row=peer)
+
+    def slot(t):
+        return t if t < SHORT else SHORT + [n for n, _, _ in DETOURS].index(t)
+
+    def leave(t):
+        return remote(a_at(2, 0, t), a_at(2, 1, t), b_send.at[3], a_recv.at[4, slot(t)], col=c - step)
+
+    def enter(t):
+        return remote(a_at(2, 0, t), a_at(2, 1, t), f_send.at[3], a_recv.at[4, slot(t)], col=c + step)
+
+    def back_other(t):
+        return remote(a_at(2, 1, t), a_at(2, 1, t), b_send.at[3], a_recv.at[4, slot(t)], col=c - step)
+
+    def over(t):
+        to = u // far
+        return remote(a_at(2, 1, t), a_at(to, 1, t), c_send, a_recv.at[to + 2, t], row=peer)
 
     def y_copy(t, side):
         at = rows_at(t, side)
@@ -334,6 +352,12 @@
 
     def take(v, side, t):
         ahead(v, side, t).wait_recv()
+
+    def take_away(t):
+        remote(a_at(2, 0, t), a_at(2, 0, t), b_send.at[1], a_recv.at[u, t], col=c - step).wait_recv()
+
+    def take_other(t):
+        enter(t).wait_recv()
 
     def within(first, t, body):
         if isinstance(t, int):
@@ -389,6 +413,9 @@
 
     @pl.when(u == 2)
     def _():
+        for t in range(SHORT):
+            enter(t).start()
+
         def both(t):
             across(t).start()
             back(2, 0, t).start()
@@ -397,7 +424,9 @@
 
     @pl.when(u == far)
     def _():
-        each(0, PIECES, lambda t: across(t).start())
+        for t, _, _ in DETOURS:
+            leave(t).start()
+        each(0, 4, lambda t: across(t).start())
 
     for j in range(2 * tiles):
         own_w(j).start()
@@ -411,16 +440,33 @@
 
         return body
 
+    def unless(t, skipped, body):
+        if isinstance(t, int):
+            if t not in skipped:
+                body()
+        elif skipped:
+            pl.when(functools.reduce(jnp.logical_and, [t != n for n in skipped]))(body)
+        else:
+            body()
+
+    def on_most(t):
+        take(0, 1, t)
+        unless(t, [n for n, _, _ in DETOURS], lambda: ahead(0, 1, t).start())
+
+    def on_back(t):
+        take_other(t)
+        back_other(t).start()
+
     def cross(t):
-        take(2, 0, t)
+        take_away(t)
         across(t).start()
 
     def pass_back(t):
-        take(2, 0, t)
+        take_away(t)
         back(2, 0, t).start()
         across(t).start()
         take(1, 1, t)
-        back(1, 1, t).start()
+        unless(t, list(range(SHORT)), lambda: back(1, 1, t).start())
 
     @pl.when(u == 0)
     def _():
@@ -434,16 +480,32 @@
         for t in range(3):
             pass_back(t)
         for t in range(2):
-            on(0, 1)(t)
+            on_most(t)
 
     @pl.when(u == 2)
     def _():
         for t in range(FILL):
             on(1, 0)(t)
+        for t, _, _ in DETOURS:
+            on_back(t)
+        on_most(0)
+
+    @pl.when(u == far)
+    def _():
+        for t in range(SHORT):
+            take_other(t)
+            over(t).start()
+        each(4, PIECES, lambda t: across(t).start())
 
     def gather(t):
         @pl.when(u == 0)
         def _():
+            for n, _, at in DETOURS:
+                @pl.when(t == at)
+                def _():
+                    take_other(n)
+                    over(n).start()
+
             within(0, t + LEAD, cross)
             within(4, t + LEAD + 4, on(0, 1))
             within(4, t + 4, send_first)
@@ -452,15 +514,20 @@
 
         @pl.when(u == 1)
         def _():
+            for n, at, _ in DETOURS:
+                @pl.when(t == at)
+                def _():
+                    on_back(n)
+                    over(n).start()
+
             within(3, t + LEAD + 3, pass_back)
             within(FILL_BACK, t + 3, send_back)
-            within(2, t + LEAD + 2, on(0, 1))
+            within(2, t + LEAD + 2, on_most)
             within(0, t + 2, on(0, 0))
             within(FILL, t + 2, send_ahead)
 
         @pl.when(u == 2)
         def _():
-            within(0, t + LEAD, on(0, 1))
             within(0, t, on(0, 0))
             within(FILL, t, on(1, 0))
             within(0, t + LEAD, lambda t: take(1, 1, t))
@@ -471,6 +538,9 @@
             within(0, t + LEAD, lambda t: take(1, 1, t))
             within(0, t, lambda t: take(0, 0, t))
             within(0, t, lambda t: take(1, 0, t))
+
+    def halfway(t):
+        pl.when(u == 2)(lambda: within(0, t + LEAD + 1, on_most))
 
     def encode(ref, at, value):
         scale = jnp.maximum(1.01 * jnp.max(jnp.abs(value), axis=1, keepdims=True), 1e-30).astype(jnp.bfloat16)
@@ -526,12 +596,12 @@
 
     def early(t):
         gather(t)
-        multiply(rows_at(t + LEAD, 1), [(t + LEAD, 1, 0)])
+        multiply(rows_at(t + LEAD, 1), [(t + LEAD, 1, 0)], lambda: halfway(t))
         reduce(t)
 
     def steady(t):
         gather(t)
-        multiply(pl.ds(pl.multiple_of(2 * t * tt, 2 * tt), 2 * tt), [(t + LEAD, 1, tt), (t, 0, 0)])
+        multiply(pl.ds(pl.multiple_of(2 * t * tt, 2 * tt), 2 * tt), [(t + LEAD, 1, tt), (t, 0, 0)], lambda: halfway(t))
         reduce(t)
 
     def late(t):
@@ -542,24 +612,54 @@
     w_all(1 - own).wait_recv()
     each(-LEAD, 0, early)
     each(0, PIECES - LEAD, steady)
-    each(PIECES - LEAD, PIECES, late)
+    each(PIECES - LEAD, PIECES - 2, late)
+    gather(PIECES - 2)
+    gather(PIECES - 1)
+    multiply(pl.ds(2 * (PIECES - 2) * tt, 4 * tt), [(PIECES - 2, 0, 0), (PIECES - 1, 0, 2 * tt)], lambda: reduce_other(PIECES - 1))
+    finish_own(PIECES - 2)
+    finish_own(PIECES - 1)
     each(PIECES, PIECES + LAG_X, finish_own)
 
     def sent(sem):
         remote(a_all(0), a_all(0), sem, a_recv.at[0, 0], row=peer).wait_send()
 
-    @pl.when(has_next)
+    def sent_few(sem, count):
+        if count:
+            some = abuf.at[0, pl.ds(0, count * tt), :]
+            remote(some, some, sem, a_recv.at[0, 0], row=peer).wait_send()
+
+    few = len(DETOURS)
+
+    @pl.when(u == 0)
     def _():
         sent(f_send.at[0])
         sent(f_send.at[2])
-        pl.when(has_last)(lambda: sent(f_send.at[1]))
+        sent_few(c_send, few)
 
     @pl.when(u == 1)
     def _():
-        sent(b_send.at[0])
-        sent(b_send.at[2])
-
-    pl.when(has_last & has_next)(lambda: sent(b_send.at[1]))
+        for n in range(2):
+            sent(f_send.at[n])
+            sent(b_send.at[n])
+        sent_few(f_send.at[2], PIECES - few)
+        sent_few(b_send.at[2], PIECES - SHORT)
+        sent_few(b_send.at[3], few)
+        sent_few(c_send, few)
+
+    @pl.when(u == 2)
+    def _():
+        for n in range(2):
+            sent(f_send.at[n])
+        sent(b_send.at[1])
+        sent_few(f_send.at[2], PIECES - few)
+        sent_few(f_send.at[3], SHORT)
+        sent_few(b_send.at[3], few)
+
+    @pl.when(u == far)
+    def _():
+        sent_few(b_send.at[3], few)
+        sent_few(c_send, SHORT)
+
     sent(c_send)
     remote(ysend, yrecv, y_send, y_recv.at[0, 0], layer=1 - l).wait_send()
     remote(xsend, xrecv, x_send, x_recv.at[0], row=peer).wait_send()
@@ -581,7 +681,7 @@
             pltpu.VMEM((3, 2 * tokens, depth), jnp.bfloat16),
             pltpu.VMEM((2, width // nc, depth, nc), jnp.bfloat16),
             pltpu.VMEM((2 * tokens, half), jnp.float32),
-            pltpu.VMEM((2 * tokens // PIECES, half), jnp.float32),
+            pltpu.VMEM((4 * tokens // PIECES, half), jnp.float32),
             pltpu.VMEM((2 * tokens, half + 128), jnp.bfloat16),
             pltpu.VMEM((2 * tokens, half + 128), jnp.bfloat16),
             pltpu.VMEM((tokens, half + 128), jnp.bfloat16),
@@ -589,8 +689,8 @@
             dma,
             dma,
             dma((5, PIECES)),
-            dma((3,)),
-            dma((3,)),
+            dma((4,)),
+            dma((4,)),
             dma,
             dma,
             dma,

time: 84.7 us -> 82.8 us (0.978)
  Pallas kernels: 83 us -> 81.7 us
    pallas_call x1, Pallas kernels: 83 us -> 81.7 us  [pair_call(): pl.pallas_call(functools.partial(pair_kernel, rows, cols), out_shape=jax....]
where the time goes in v4:
time: 82.8 us; the launch traced here: 82.6 us
  Pallas kernels  81.7 us (99%)
  local copies, waits for them, and re-layouts  0.97 us (1%)
    pallas_call x1, Pallas kernels, pair_call(): pl.pallas_call(functools.partial(pair_kernel, rows, cols), out_shape=jax....  81.7 us

profile of v4, /device:TPU:0, one launch (start us, length us, event | category | flops | bytes accessed | tf_op | source)
XLA Modules:
  0.0 82.6 jit_solution(10856069926877360024)
XLA Ops:
  0.0 81.7 %shard_map.28 = bf16[512,1024]{1,0:T(8,128)(2,1)S(1)} custom-call(bf16[512,1024]{1,0:T(8,128)(2,1)} %a_ref.1, bf16[1024,2048]{1,0:T(8,128)(2,1)} %w_ref.1), custom_call_target="tpu_custom_call" | custom-call | tf_op jit(solution)/shard_map/pallas_call | solution.py:675
  81.7 1.0 %copy.4 = bf16[512,1024]{1,0:T(8,128)(2,1)} copy(bf16[512,1024]{1,0:T(8,128)(2,1)S(1)} %shard_map.28) | data formatting | bytes 2097152

commit v5 on v4

--- a/solution.py
+++ b/solution.py
@@ -267,7 +267,7 @@
 
 
 PIECES = 16
-DETOURS = ((12, 2, 5), (14, 4, 7))
+DETOURS = ((12, 0, 6), (14, 1, 8))
 SHORT = 2
 FILL = 6
 FILL_BACK = 3
@@ -400,6 +400,10 @@
 
         lax.fori_loop(start, stop, one, 0)
 
+    def both(t):
+        across(t).start()
+        back(2, 0, t).start()
+
     @pl.when(u == 0)
     def _():
         each(0, 2, send_first)
@@ -416,11 +420,7 @@
         for t in range(SHORT):
             enter(t).start()
 
-        def both(t):
-            across(t).start()
-            back(2, 0, t).start()
-
-        each(0, PIECES, both)
+        each(0, FILL, both)
 
     @pl.when(u == far)
     def _():
@@ -486,8 +486,10 @@
     def _():
         for t in range(FILL):
             on(1, 0)(t)
-        for t, _, _ in DETOURS:
-            on_back(t)
+            if t == 1:
+                for n, _, _ in DETOURS:
+                    on_back(n)
+                each(FILL, PIECES, both)
         on_most(0)
 
     @pl.when(u == far)

time: 82.8 us -> 82.4 us (level)
  no operation moved by 1% of the time
where the time goes in v5:
time: 82.4 us; the launch traced here: 82.2 us
  Pallas kernels  81.3 us (99%)
  local copies, waits for them, and re-layouts  0.97 us (1%)
    pallas_call x1, Pallas kernels, pair_call(): pl.pallas_call(functools.partial(pair_kernel, rows, cols), out_shape=jax....  81.3 us

profile of v5, /device:TPU:0, one launch (start us, length us, event | category | flops | bytes accessed | tf_op | source)
XLA Modules:
  0.0 82.2 jit_solution(4389101919796279434)
XLA Ops:
  0.0 81.3 %shard_map.28 = bf16[512,1024]{1,0:T(8,128)(2,1)S(1)} custom-call(bf16[512,1024]{1,0:T(8,128)(2,1)} %a_ref.1, bf16[1024,2048]{1,0:T(8,128)(2,1)} %w_ref.1), custom_call_target="tpu_custom_call" | custom-call | tf_op jit(solution)/shard_map/pallas_call | solution.py:677
  81.3 1.0 %copy.4 = bf16[512,1024]{1,0:T(8,128)(2,1)} copy(bf16[512,1024]{1,0:T(8,128)(2,1)S(1)} %shard_map.28) | data formatting | bytes 2097152

commit v6 on v5

--- a/solution.py
+++ b/solution.py
@@ -278,7 +278,7 @@
 SPAN = 250.0
 
 
-def pair_kernel(rows, cols, a_ref, w_ref, o_ref, abuf, wbuf, acc, part, ysend, yrecv, xsend, xrecv, loc_a, loc_w, a_recv, f_send, b_send, c_send, w_send, w_recv, y_send, y_recv, x_send, x_recv):
+def pair_kernel(rows, cols, a_ref, w_ref, o_ref, abuf, wbuf, acc, part, ysend, yrecv, xsend, xrecv, loc_a, loc_w, a_recv, o_recv, f_send, b_send, c_send, w_send, w_recv, y_send, y_recv, x_send, x_recv):
     r, c, l = lax.axis_index("row"), lax.axis_index("col"), lax.axis_index("layer")
     x, core = r // 2, lax.rem(r, 2)
     partner, peer = 2 * x + 1 - core, 2 * (1 - x) + core
@@ -330,13 +330,13 @@
         return t if t < SHORT else SHORT + [n for n, _, _ in DETOURS].index(t)
 
     def leave(t):
-        return remote(a_at(2, 0, t), a_at(2, 1, t), b_send.at[3], a_recv.at[4, slot(t)], col=c - step)
+        return remote(a_at(2, 0, t), a_at(2, 1, t), b_send.at[3], o_recv.at[slot(t)], col=c - step)
 
     def enter(t):
-        return remote(a_at(2, 0, t), a_at(2, 1, t), f_send.at[3], a_recv.at[4, slot(t)], col=c + step)
+        return remote(a_at(2, 0, t), a_at(2, 1, t), f_send.at[3], o_recv.at[slot(t)], col=c + step)
 
     def back_other(t):
-        return remote(a_at(2, 1, t), a_at(2, 1, t), b_send.at[3], a_recv.at[4, slot(t)], col=c - step)
+        return remote(a_at(2, 1, t), a_at(2, 1, t), b_send.at[3], o_recv.at[slot(t)], col=c - step)
 
     def over(t):
         to = u // far
@@ -690,7 +690,8 @@
             pltpu.VMEM((tokens, half + 128), jnp.bfloat16),
             dma,
             dma,
-            dma((5, PIECES)),
+            dma((4, PIECES)),
+            dma((SHORT + len(DETOURS),)),
             dma((4,)),
             dma((4,)),
             dma,
@@ -705,11 +706,18 @@
     )(*(pltpu.with_memory_space_constraint(v, pltpu.HBM) for v in (attn_values, out_weight)))
 
 
+def pairs_up(rows, cols, attn_values, out_weight):
+    groups, depth = rows // 2, attn_values.shape[1]
+    same = cols == 2 * groups and depth == out_weight.shape[0]
+    whole = attn_values.shape[0] % (16 * PIECES) == 0 and out_weight.shape[1] % 1024 == 0
+    return groups == 2 and same and whole
+
+
 def solution(mesh):
     rows, cols = mesh.shape["row"], mesh.shape["col"]
 
     def shards(attn_values, out_weight):
-        if rows == cols == 4:
+        if pairs_up(rows, cols, attn_values, out_weight):
             return pair_call(rows, cols, attn_values, out_weight)
         tokens, depth_a = attn_values.shape
         depth_w, width = out_weight.shape

time: 82.4 us -> 82.3 us (level)
  no operation moved by 1% of the time
where the time goes in v6:
time: 82.3 us; the launch traced here: 82.1 us
  Pallas kernels  81.2 us (99%)
  local copies, waits for them, and re-layouts  0.97 us (1%)
    pallas_call x1, Pallas kernels, pair_call(): pl.pallas_call(functools.partial(pair_kernel, rows, cols), out_shape=jax....  81.2 us

profile of v6, /device:TPU:0, one launch (start us, length us, event | category | flops | bytes accessed | tf_op | source)
XLA Modules:
  0.0 82.1 jit_solution(652352471484985949)
XLA Ops:
  0.0 81.2 %shard_map.28 = bf16[512,1024]{1,0:T(8,128)(2,1)S(1)} custom-call(bf16[512,1024]{1,0:T(8,128)(2,1)} %a_ref.1, bf16[1024,2048]{1,0:T(8,128)(2,1)} %w_ref.1), custom_call_target="tpu_custom_call" | custom-call | tf_op jit(solution)/shard_map/pallas_call | solution.py:677
  81.2 1.0 %copy.4 = bf16[512,1024]{1,0:T(8,128)(2,1)} copy(bf16[512,1024]{1,0:T(8,128)(2,1)S(1)} %shard_map.28) | data formatting | bytes 2097152

commit v7 on v6

--- a/solution.py
+++ b/solution.py
@@ -268,7 +268,7 @@
 
 PIECES = 16
 DETOURS = ((12, 0, 6), (14, 1, 8))
-SHORT = 2
+SHORT = 3
 FILL = 6
 FILL_BACK = 3
 LEAD = 3
@@ -461,10 +461,13 @@
         take_away(t)
         across(t).start()
 
-    def pass_back(t):
+    def away(t):
         take_away(t)
         back(2, 0, t).start()
         across(t).start()
+
+    def pass_back(t):
+        within(1, t + 1, away)
         take(1, 1, t)
         unless(t, list(range(SHORT)), lambda: back(1, 1, t).start())
 
@@ -474,9 +477,11 @@
             on(0, 1)(t)
             if t >= 2:
                 send_first(t)
+        cross(0)
 
     @pl.when(u == 1)
     def _():
+        away(0)
         for t in range(3):
             pass_back(t)
         for t in range(2):
@@ -508,7 +513,7 @@
                     take_other(n)
                     over(n).start()
 
-            within(0, t + LEAD, cross)
+            within(1, t + LEAD + 1, cross)
             within(4, t + LEAD + 4, on(0, 1))
             within(4, t + 4, send_first)
             within(0, t + LEAD, lambda t: take(1, 1, t))

time: 82.3 us -> 82.4 us (level)
  no operation moved by 1% of the time
where the time goes in v7:
time: 82.4 us; the launch traced here: 82.2 us
  Pallas kernels  81.3 us (99%)
  local copies, waits for them, and re-layouts  0.97 us (1%)
    pallas_call x1, Pallas kernels, pair_call(): pl.pallas_call(functools.partial(pair_kernel, rows, cols), out_shape=jax....  81.3 us

profile of v7, /device:TPU:0, one launch (start us, length us, event | category | flops | bytes accessed | tf_op | source)
XLA Modules:
  0.0 82.2 jit_solution(345260915381303881)
XLA Ops:
  0.0 81.3 %shard_map.28 = bf16[512,1024]{1,0:T(8,128)(2,1)S(1)} custom-call(bf16[512,1024]{1,0:T(8,128)(2,1)} %a_ref.1, bf16[1024,2048]{1,0:T(8,128)(2,1)} %w_ref.1), custom_call_target="tpu_custom_call" | custom-call | tf_op jit(solution)/shard_map/pallas_call | solution.py:682
  81.3 1.0 %copy.4 = bf16[512,1024]{1,0:T(8,128)(2,1)} copy(bf16[512,1024]{1,0:T(8,128)(2,1)S(1)} %shard_map.28) | data formatting | bytes 2097152
